TPU v7x, 32 devices: a whole 2x2x4 slice. The times are simulated.
32 devices in a mesh: seqa: 8 (over z, x), seqb: 4 (over y, core).
Axes of the slice: x: 2, y: 2, z: 4, core: 2. Of those that a mesh axis runs over, the one named last changes fastest.
Arguments:
- queries: bfloat16 [16384, 4096], P(('seqa', 'seqb')), may hold values from -60 to 60
- keys: bfloat16 [16384, 1024], P(('seqa', 'seqb')), may hold values from -8 to 8
- values: bfloat16 [16384, 1024], P(('seqa', 'seqb')), may hold values from -6 to 6
- doc_start: int32 [16384], P(('seqa', 'seqb')), may hold values from 0 to 16383, as said below
Outputs:
- attended: bfloat16 [16384, 4096], P(('seqa', 'seqb'))
Inputs may be any that keep to these rules, and one draw needn't show every extreme that they name: Never falling along the sequence, doc_start[i] <= i, the same value for all tokens of one document, and doc_start[0] = 0.
All inputs are finite; a program needn't handle non-finite values.
Results may differ from a plain program's by a relative error of at most 0.0038.
Values may be sent and summed in bfloat16 or wider, within the bound.
A program may use at most 64 MiB of HBM per device.

v0:
```python
import math

import jax
import jax.numpy as jnp
from jax import lax
from jax.sharding import PartitionSpec as P

HEAD_SIZE = 128


def passed_along(block, axis, distance):
    devices = range(lax.axis_size(axis))
    route = [(i - distance, i) for i in devices if i - distance in devices]
    return lax.ppermute(block, axis, route)


def attend_block(
    block_of_queries, block_of_keys, block_of_values, query_place, key_place, starts, window_length
):
    score_scale = 1.0 / math.sqrt(block_of_queries.shape[-1])
    scores = (
        jnp.einsum(
            "tgd,kd->gtk", block_of_queries, block_of_keys, preferred_element_type=jnp.float32
        )
        * score_scale
    )
    visible = (
        (key_place[None, :] <= query_place[:, None])
        & (key_place[None, :] > query_place[:, None] - window_length)
        & (key_place[None, :] >= starts[:, None])
    )
    scores = jnp.where(visible[None], scores, jnp.float32(-1e30))
    row_top = jnp.max(scores, axis=-1, keepdims=True)
    exponent = jnp.where(visible[None], jnp.exp(scores - row_top), jnp.float32(0.0))
    row_sum = jnp.sum(exponent, axis=-1, keepdims=True)
    weights = exponent.astype(jnp.bfloat16)
    summed = jnp.einsum("gtk,kd->tgd", weights, block_of_values, preferred_element_type=jnp.float32)
    return summed / jnp.transpose(row_sum, (1, 0, 2))


def local(queries, keys, values, doc_start):
    shard_rows = queries.shape[0]
    head_width = HEAD_SIZE
    group_width = queries.shape[1] // keys.shape[1]
    kv_heads = keys.shape[1] // head_width
    key_value = (keys, values)
    first_back = passed_along((key_value[0], key_value[1]), ("seqa", "seqb"), 1)
    second_back = passed_along((key_value[0], key_value[1]), ("seqa", "seqb"), 2)
    key_all = jnp.concatenate([second_back[0], first_back[0], keys], axis=0)
    value_all = jnp.concatenate([second_back[1], first_back[1], values], axis=0)
    window_length = 2 * shard_rows
    rows_per_block = min(512, shard_rows)
    block_count = shard_rows // rows_per_block
    shard_start = lax.axis_index(("seqa", "seqb")) * shard_rows

    def one_step(step_index, output):
        kv_head = step_index // block_count
        offset = step_index % block_count * rows_per_block
        block_of_queries = lax.dynamic_slice(
            queries,
            (offset, kv_head * group_width * head_width),
            (rows_per_block, group_width * head_width),
        )
        block_of_queries = block_of_queries.reshape(rows_per_block, group_width, head_width)
        block_of_keys = lax.dynamic_slice(
            key_all, (offset, kv_head * head_width), (window_length + rows_per_block, head_width)
        )
        block_of_values = lax.dynamic_slice(
            value_all, (offset, kv_head * head_width), (window_length + rows_per_block, head_width)
        )
        query_place = shard_start + offset + jnp.arange(rows_per_block, dtype=jnp.int32)
        key_place = (
            shard_start
            - window_length
            + offset
            + jnp.arange(window_length + rows_per_block, dtype=jnp.int32)
        )
        attended_block = attend_block(
            block_of_queries,
            block_of_keys,
            block_of_values,
            query_place,
            key_place,
            doc_start,
            window_length,
        )
        attended_block = attended_block.reshape(rows_per_block, group_width * head_width).astype(
            jnp.bfloat16
        )
        return lax.dynamic_update_slice(
            output, attended_block, (offset, kv_head * group_width * head_width)
        )

    return lax.fori_loop(0, kv_heads * block_count, one_step, jnp.zeros_like(queries))


def solution(mesh):
    return jax.shard_map(
        local,
        mesh=mesh,
        in_specs=(
            P(("seqa", "seqb"), None),
            P(("seqa", "seqb"), None),
            P(("seqa", "seqb"), None),
            P(("seqa", "seqb")),
        ),
        out_specs=P(("seqa", "seqb"), None),
        check_vma=False,
    )
```

profile of v0, /device:TPU:8, one launch (start us, length us, event | category | flops | bytes accessed | tf_op | source)
XLA Modules:
  0.0 212.1 jit_solution(15962611218056392615)
XLA Ops:
  0.0 1.6 copy.12
  1.6 1.9 collective-permute-start.1
  3.5 3.4 %collective-permute-start = (bf16[512,1024]{0,1:T(8,128)(2,1)S(1)}, bf16[512,1024]{0,1:T(8,128)(2,1)}, u32[]{:S(2)}, u32[]{:S(2)}) collective-permute-start(bf16[512,1024]{0,1:T(8,128)(2,1)S(1)} %copy.12), channel_id=1, source_target_pairs={{0,2},{1,3},{2,4},{3,5},{4,6},{5,7},{6,8},{7,9},{8,10},{9,11},{10,... | collective-permute-start | bytes 3145736 | tf_op jit(solution)/shard_map/ppermute | solution.py:14
  7.0 3.3 %collective-permute-start.2 = (bf16[512,1024]{1,0:T(8,128)(2,1)}, bf16[512,1024]{1,0:T(8,128)(2,1)S(1)}, u32[]{:S(2)}, u32[]{:S(2)}) collective-permute-start(bf16[512,1024]{1,0:T(8,128)(2,1)} %param.7), channel_id=1, source_target_pairs={{0,2},{1,3},{2,4},{3,5},{4,6},{5,7},{6,8},{7,9},{8,10},{9,11},{10,... | collective-permute-start | bytes 3145736 | tf_op jit(solution)/shard_map/ppermute | solution.py:14
  10.3 3.0 %collective-permute-start.3 = (bf16[512,1024]{1,0:T(8,128)(2,1)}, bf16[512,1024]{1,0:T(8,128)(2,1)}, u32[]{:S(2)}, u32[]{:S(2)}) collective-permute-start(bf16[512,1024]{1,0:T(8,128)(2,1)} %param.7), channel_id=1, source_target_pairs={{0,1},{1,2},{2,3},{3,4},{4,5},{5,6},{6,7},{7,8},{8,9},{9,10},{10,1... | collective-permute-start | bytes 3145736 | tf_op jit(solution)/shard_map/ppermute | solution.py:14
  13.3 15.0 %collective-permute-done.1 = bf16[512,1024]{0,1:T(8,128)(2,1)} collective-permute-done((bf16[512,1024]{0,1:T(8,128)(2,1)S(1)}, bf16[512,1024]{0,1:T(8,128)(2,1)}, u32[]{:S(2)}, u32[]{:S(2)}) %collective-permute-start.1) | collective-permute-done | bytes 1048608 | tf_op jit(solution)/shard_map/ppermute | solution.py:14
  28.3 5.0 %collective-permute-done = bf16[512,1024]{0,1:T(8,128)(2,1)} collective-permute-done((bf16[512,1024]{0,1:T(8,128)(2,1)S(1)}, bf16[512,1024]{0,1:T(8,128)(2,1)}, u32[]{:S(2)}, u32[]{:S(2)}) %collective-permute-start) | collective-permute-done | bytes 1048608 | tf_op jit(solution)/shard_map/ppermute | solution.py:14
  33.4 3.0 %pad_maximum_fusion = bf16[1536,1024]{0,1:T(8,128)(2,1)} fusion(bf16[512,1024]{0,1:T(8,128)(2,1)S(1)} %copy.12, bf16[512,1024]{0,1:T(8,128)(2,1)} %collective-permute-done.1, bf16[512,1024]{0,1:T(8,128)(2,1)} %collective-permute-done), kind=kLoop, calls=%fused_computation.31 | loop fusion | flops 9437184 | bytes 6291456 | tf_op jit(solution)/shard_map/concatenate | solution.py:50
  36.4 19.4 %collective-permute-done.2 = bf16[512,1024]{1,0:T(8,128)(2,1)S(1)} collective-permute-done((bf16[512,1024]{1,0:T(8,128)(2,1)}, bf16[512,1024]{1,0:T(8,128)(2,1)S(1)}, u32[]{:S(2)}, u32[]{:S(2)}) %collective-permute-start.2) | collective-permute-done | bytes 1048608 | tf_op jit(solution)/shard_map/ppermute | solution.py:14
  55.7 20.1 %collective-permute-done.3 = bf16[512,1024]{1,0:T(8,128)(2,1)} collective-permute-done((bf16[512,1024]{1,0:T(8,128)(2,1)}, bf16[512,1024]{1,0:T(8,128)(2,1)}, u32[]{:S(2)}, u32[]{:S(2)}) %collective-permute-start.3) | collective-permute-done | bytes 1048608 | tf_op jit(solution)/shard_map/ppermute | solution.py:14
  75.8 2.9 %pad_maximum_fusion.1 = bf16[1536,1024]{1,0:T(8,128)(2,1)} fusion(bf16[512,1024]{1,0:T(8,128)(2,1)S(1)} %copy-done, bf16[512,1024]{1,0:T(8,128)(2,1)} %collective-permute-done.3, bf16[512,1024]{1,0:T(8,128)(2,1)S(1)} %collective-permute-done.2), kind=kLoop, calls=%fused_computation.32 | loop fusion | flops 9437184 | bytes 6291456 | tf_op jit(solution)/shard_map/concatenate | solution.py:49
  78.6 2.5 %broadcast_in_dim.82.clone = bf16[512,4096]{1,0:T(8,128)(2,1)} broadcast(bf16[]{:T(256)} %constant.186.clone.1), dimensions={} | broadcast | bytes 4194306 | tf_op jit(solution)/shard_map/broadcast_in_dim | solution.py:94
  81.2 131.0 %while.16 = (s32[]{:T(128)}, bf16[512,4096]{1,0:T(8,128)(2,1)}, bf16[1536,1024]{0,1:T(8,128)(2,1)}, s32[]{:T(128)}, s32[]{:T(128)}, /*index=5*/s32[512]{0:T(512)...) while((s32[]{:T(128)}, bf16[512,4096]{1,0:T(8,128)(2,1)}, ...), condition=%wide.region_3.4_spmd, body=%wide.region_0.3_spmd.sunk | while | flops 1633947648 | bytes 21010688 | solution.py:94
  82.5 1.2 compare_and_fusion.2
  83.6 8.9 %fusion.56 = (f32[4,512]{1,0:T(4,128)S(1)}, bf16[4,512,1536]{1,2,0:T(8,128)(2,1)}) fusion(pred[512,1536]{0,1:T(8,128)(4,1)S(1)} %compare_and_fusion.2, bf16[512,4,128]{0,2,1:T(8,128)(2,1)S(1)} %bitcast.61, bf16[1536,1024]{1,0:T(8,128)(2,1)} %get-tuple-element.346, s32[]{:T(128)S(6)} %select_n.95), kind=kOutput, calls=%fused_computation.33.clone.1 | convolution fusion | flops 824182272 | bytes 8790020 | tf_op jit(solution)/shard_map/while/body/eval_jaxpr/sub | solution.py:34
  92.6 3.9 %fusion.57 = bf16[512,4,128]{0,2,1:T(8,128)(2,1)S(1)} fusion(bf16[4,512,1536]{1,2,0:T(8,128)(2,1)} %get-tuple-element.310, f32[512,4]{0,1:T(4,128)S(1)} %bitcast.63, bf16[1536,1024]{0,1:T(8,128)(2,1)} %get-tuple-element.342, s32[]{:T(128)S(6)} %select_n.95), kind=kOutput, calls=%fused_computation.13.clone.1 | convolution fusion | flops 805830656 | bytes 7217156 | tf_op jit(solution)/shard_map/while/body/eval_jaxpr/gtk,kd->tgd/dot_general | solution.py:37
  98.9 1.2 compare_and_fusion.2
  100.0 8.9 %fusion.56 = (f32[4,512]{1,0:T(4,128)S(1)}, bf16[4,512,1536]{1,2,0:T(8,128)(2,1)}) fusion(pred[512,1536]{0,1:T(8,128)(4,1)S(1)} %compare_and_fusion.2, bf16[512,4,128]{0,2,1:T(8,128)(2,1)S(1)} %bitcast.61, bf16[1536,1024]{1,0:T(8,128)(2,1)} %get-tuple-element.346, s32[]{:T(128)S(6)} %select_n.95), kind=kOutput, calls=%fused_computation.33.clone.1 | convolution fusion | flops 824182272 | bytes 8790020 | tf_op jit(solution)/shard_map/while/body/eval_jaxpr/sub | solution.py:34
  108.9 3.9 %fusion.57 = bf16[512,4,128]{0,2,1:T(8,128)(2,1)S(1)} fusion(bf16[4,512,1536]{1,2,0:T(8,128)(2,1)} %get-tuple-element.310, f32[512,4]{0,1:T(4,128)S(1)} %bitcast.63, bf16[1536,1024]{0,1:T(8,128)(2,1)} %get-tuple-element.342, s32[]{:T(128)S(6)} %select_n.95), kind=kOutput, calls=%fused_computation.13.clone.1 | convolution fusion | flops 805830656 | bytes 7217156 | tf_op jit(solution)/shard_map/while/body/eval_jaxpr/gtk,kd->tgd/dot_general | solution.py:37
  115.2 1.2 compare_and_fusion.2
  116.4 8.9 %fusion.56 = (f32[4,512]{1,0:T(4,128)S(1)}, bf16[4,512,1536]{1,2,0:T(8,128)(2,1)}) fusion(pred[512,1536]{0,1:T(8,128)(4,1)S(1)} %compare_and_fusion.2, bf16[512,4,128]{0,2,1:T(8,128)(2,1)S(1)} %bitcast.61, bf16[1536,1024]{1,0:T(8,128)(2,1)} %get-tuple-element.346, s32[]{:T(128)S(6)} %select_n.95), kind=kOutput, calls=%fused_computation.33.clone.1 | convolution fusion | flops 824182272 | bytes 8790020 | tf_op jit(solution)/shard_map/while/body/eval_jaxpr/sub | solution.py:34
  125.3 3.9 %fusion.57 = bf16[512,4,128]{0,2,1:T(8,128)(2,1)S(1)} fusion(bf16[4,512,1536]{1,2,0:T(8,128)(2,1)} %get-tuple-element.310, f32[512,4]{0,1:T(4,128)S(1)} %bitcast.63, bf16[1536,1024]{0,1:T(8,128)(2,1)} %get-tuple-element.342, s32[]{:T(128)S(6)} %select_n.95), kind=kOutput, calls=%fused_computation.13.clone.1 | convolution fusion | flops 805830656 | bytes 7217156 | tf_op jit(solution)/shard_map/while/body/eval_jaxpr/gtk,kd->tgd/dot_general | solution.py:37
  132.8 8.9 %fusion.56 = (f32[4,512]{1,0:T(4,128)S(1)}, bf16[4,512,1536]{1,2,0:T(8,128)(2,1)}) fusion(pred[512,1536]{0,1:T(8,128)(4,1)S(1)} %compare_and_fusion.2, bf16[512,4,128]{0,2,1:T(8,128)(2,1)S(1)} %bitcast.61, bf16[1536,1024]{1,0:T(8,128)(2,1)} %get-tuple-element.346, s32[]{:T(128)S(6)} %select_n.95), kind=kOutput, calls=%fused_computation.33.clone.1 | convolution fusion | flops 824182272 | bytes 8790020 | tf_op jit(solution)/shard_map/while/body/eval_jaxpr/sub | solution.py:34
  141.7 3.9 %fusion.57 = bf16[512,4,128]{0,2,1:T(8,128)(2,1)S(1)} fusion(bf16[4,512,1536]{1,2,0:T(8,128)(2,1)} %get-tuple-element.310, f32[512,4]{0,1:T(4,128)S(1)} %bitcast.63, bf16[1536,1024]{0,1:T(8,128)(2,1)} %get-tuple-element.342, s32[]{:T(128)S(6)} %select_n.95), kind=kOutput, calls=%fused_computation.13.clone.1 | convolution fusion | flops 805830656 | bytes 7217156 | tf_op jit(solution)/shard_map/while/body/eval_jaxpr/gtk,kd->tgd/dot_general | solution.py:37
  149.1 8.9 %fusion.56 = (f32[4,512]{1,0:T(4,128)S(1)}, bf16[4,512,1536]{1,2,0:T(8,128)(2,1)}) fusion(pred[512,1536]{0,1:T(8,128)(4,1)S(1)} %compare_and_fusion.2, bf16[512,4,128]{0,2,1:T(8,128)(2,1)S(1)} %bitcast.61, bf16[1536,1024]{1,0:T(8,128)(2,1)} %get-tuple-element.346, s32[]{:T(128)S(6)} %select_n.95), kind=kOutput, calls=%fused_computation.33.clone.1 | convolution fusion | flops 824182272 | bytes 8790020 | tf_op jit(solution)/shard_map/while/body/eval_jaxpr/sub | solution.py:34
  158.1 3.9 %fusion.57 = bf16[512,4,128]{0,2,1:T(8,128)(2,1)S(1)} fusion(bf16[4,512,1536]{1,2,0:T(8,128)(2,1)} %get-tuple-element.310, f32[512,4]{0,1:T(4,128)S(1)} %bitcast.63, bf16[1536,1024]{0,1:T(8,128)(2,1)} %get-tuple-element.342, s32[]{:T(128)S(6)} %select_n.95), kind=kOutput, calls=%fused_computation.13.clone.1 | convolution fusion | flops 805830656 | bytes 7217156 | tf_op jit(solution)/shard_map/while/body/eval_jaxpr/gtk,kd->tgd/dot_general | solution.py:37
  165.5 8.9 %fusion.56 = (f32[4,512]{1,0:T(4,128)S(1)}, bf16[4,512,1536]{1,2,0:T(8,128)(2,1)}) fusion(pred[512,1536]{0,1:T(8,128)(4,1)S(1)} %compare_and_fusion.2, bf16[512,4,128]{0,2,1:T(8,128)(2,1)S(1)} %bitcast.61, bf16[1536,1024]{1,0:T(8,128)(2,1)} %get-tuple-element.346, s32[]{:T(128)S(6)} %select_n.95), kind=kOutput, calls=%fused_computation.33.clone.1 | convolution fusion | flops 824182272 | bytes 8790020 | tf_op jit(solution)/shard_map/while/body/eval_jaxpr/sub | solution.py:34
  174.4 3.9 %fusion.57 = bf16[512,4,128]{0,2,1:T(8,128)(2,1)S(1)} fusion(bf16[4,512,1536]{1,2,0:T(8,128)(2,1)} %get-tuple-element.310, f32[512,4]{0,1:T(4,128)S(1)} %bitcast.63, bf16[1536,1024]{0,1:T(8,128)(2,1)} %get-tuple-element.342, s32[]{:T(128)S(6)} %select_n.95), kind=kOutput, calls=%fused_computation.13.clone.1 | convolution fusion | flops 805830656 | bytes 7217156 | tf_op jit(solution)/shard_map/while/body/eval_jaxpr/gtk,kd->tgd/dot_general | solution.py:37
  181.9 8.9 %fusion.56 = (f32[4,512]{1,0:T(4,128)S(1)}, bf16[4,512,1536]{1,2,0:T(8,128)(2,1)}) fusion(pred[512,1536]{0,1:T(8,128)(4,1)S(1)} %compare_and_fusion.2, bf16[512,4,128]{0,2,1:T(8,128)(2,1)S(1)} %bitcast.61, bf16[1536,1024]{1,0:T(8,128)(2,1)} %get-tuple-element.346, s32[]{:T(128)S(6)} %select_n.95), kind=kOutput, calls=%fused_computation.33.clone.1 | convolution fusion | flops 824182272 | bytes 8790020 | tf_op jit(solution)/shard_map/while/body/eval_jaxpr/sub | solution.py:34
  190.8 3.9 %fusion.57 = bf16[512,4,128]{0,2,1:T(8,128)(2,1)S(1)} fusion(bf16[4,512,1536]{1,2,0:T(8,128)(2,1)} %get-tuple-element.310, f32[512,4]{0,1:T(4,128)S(1)} %bitcast.63, bf16[1536,1024]{0,1:T(8,128)(2,1)} %get-tuple-element.342, s32[]{:T(128)S(6)} %select_n.95), kind=kOutput, calls=%fused_computation.13.clone.1 | convolution fusion | flops 805830656 | bytes 7217156 | tf_op jit(solution)/shard_map/while/body/eval_jaxpr/gtk,kd->tgd/dot_general | solution.py:37
  198.2 8.9 %fusion.56 = (f32[4,512]{1,0:T(4,128)S(1)}, bf16[4,512,1536]{1,2,0:T(8,128)(2,1)}) fusion(pred[512,1536]{0,1:T(8,128)(4,1)S(1)} %compare_and_fusion.2, bf16[512,4,128]{0,2,1:T(8,128)(2,1)S(1)} %bitcast.61, bf16[1536,1024]{1,0:T(8,128)(2,1)} %get-tuple-element.346, s32[]{:T(128)S(6)} %select_n.95), kind=kOutput, calls=%fused_computation.33.clone.1 | convolution fusion | flops 824182272 | bytes 8790020 | tf_op jit(solution)/shard_map/while/body/eval_jaxpr/sub | solution.py:34
  207.2 3.9 %fusion.57 = bf16[512,4,128]{0,2,1:T(8,128)(2,1)S(1)} fusion(bf16[4,512,1536]{1,2,0:T(8,128)(2,1)} %get-tuple-element.310, f32[512,4]{0,1:T(4,128)S(1)} %bitcast.63, bf16[1536,1024]{0,1:T(8,128)(2,1)} %get-tuple-element.342, s32[]{:T(128)S(6)} %select_n.95), kind=kOutput, calls=%fused_computation.13.clone.1 | convolution fusion | flops 805830656 | bytes 7217156 | tf_op jit(solution)/shard_map/while/body/eval_jaxpr/gtk,kd->tgd/dot_general | solution.py:37
  (57 shorter events, 24.5 us)
Async XLA Ops:
  0.0 75.8 %copy-start = (bf16[512,1024]{1,0:T(8,128)(2,1)S(1)}, bf16[512,1024]{1,0:T(8,128)(2,1)}, u32[]{:S(2)}) copy-start(bf16[512,1024]{1,0:T(8,128)(2,1)} %param.7) | copy-start | bytes 3145732
  1.6 26.8 %collective-permute-start.1 = (bf16[512,1024]{0,1:T(8,128)(2,1)S(1)}, bf16[512,1024]{0,1:T(8,128)(2,1)}, u32[]{:S(2)}, u32[]{:S(2)}) collective-permute-start(bf16[512,1024]{0,1:T(8,128)(2,1)S(1)} %copy.12), channel_id=1, source_target_pairs={{0,1},{1,2},{2,3},{3,4},{4,5},{5,6},{6,7},{7,8},{8,9},{9,10},{10,1... | collective-permute-start | bytes 3145736 | tf_op jit(solution)/shard_map/ppermute | solution.py:14
  3.5 29.8 %collective-permute-start = (bf16[512,1024]{0,1:T(8,128)(2,1)S(1)}, bf16[512,1024]{0,1:T(8,128)(2,1)}, u32[]{:S(2)}, u32[]{:S(2)}) collective-permute-start(bf16[512,1024]{0,1:T(8,128)(2,1)S(1)} %copy.12), channel_id=1, source_target_pairs={{0,2},{1,3},{2,4},{3,5},{4,6},{5,7},{6,8},{7,9},{8,10},{9,11},{10,... | collective-permute-start | bytes 3145736 | tf_op jit(solution)/shard_map/ppermute | solution.py:14
  7.0 48.8 %collective-permute-start.2 = (bf16[512,1024]{1,0:T(8,128)(2,1)}, bf16[512,1024]{1,0:T(8,128)(2,1)S(1)}, u32[]{:S(2)}, u32[]{:S(2)}) collective-permute-start(bf16[512,1024]{1,0:T(8,128)(2,1)} %param.7), channel_id=1, source_target_pairs={{0,2},{1,3},{2,4},{3,5},{4,6},{5,7},{6,8},{7,9},{8,10},{9,11},{10,... | collective-permute-start | bytes 3145736 | tf_op jit(solution)/shard_map/ppermute | solution.py:14
  10.3 65.5 %collective-permute-start.3 = (bf16[512,1024]{1,0:T(8,128)(2,1)}, bf16[512,1024]{1,0:T(8,128)(2,1)}, u32[]{:S(2)}, u32[]{:S(2)}) collective-permute-start(bf16[512,1024]{1,0:T(8,128)(2,1)} %param.7), channel_id=1, source_target_pairs={{0,1},{1,2},{2,3},{3,4},{4,5},{5,6},{6,7},{7,8},{8,9},{9,10},{10,1... | collective-permute-start | bytes 3145736 | tf_op jit(solution)/shard_map/ppermute | solution.py:14
  36.4 44.8 %copy-start.1 = (s32[512]{0:T(512)S(1)}, s32[512]{0:T(512)}, u32[]{:S(2)}) copy-start(s32[512]{0:T(512)} %param.9) | copy-start | bytes 6148
where the time goes:
time: 213 us; the launch traced here: 212 us
  matrix products  103 us (48%)
  waiting for transfers between devices  59.5 us (28%)
  local copies, waits for them, and re-layouts  22.8 us (11%)
  other arithmetic  15.2 us (7%)
  starting transfers between devices  11.7 us (5%)
    sub x8, matrix products, attend_block(): scores - row_top  71.3 us
    ppermute x4, waiting for transfers between devices, passed_along(): return lax.ppermute(block, axis, route)  59.5 us
    dot_general x8, matrix products, attend_block(): jnp.einsum('gtk,kd->tgd', weights, block_of_values, preferred_element_typ...  31.4 us
    ppermute x4, starting transfers between devices, passed_along(): return lax.ppermute(block, axis, route)  11.7 us
    dynamic_slice x16, local copies, waits for them, and re-layouts, one_step(): lax.dynamic_slice(queries, (offset, kv_head * group_width * head_width),...  10.3 us
    and x8, other arithmetic, attend_block(): (key_place[None, :] <= query_place[:, None]) & (key_place[None, :] > quer...  9.27 us
    dynamic_update_slice x16, local copies, waits for them, and re-layouts, one_step(): lax.dynamic_update_slice(output, attended_block, (offset, kv_head * group...  8.37 us
  transfers between devices with their start and end apart: 4, of which 4 were waited for; matrix products, arithmetic and copies ran while one was open for 1% of the time, Pallas kernels for 0%

commit v1 on v0

v1 whole, which is shorter than its diff:
```python
import functools
import math

import jax
import jax.numpy as jnp
from jax import lax
from jax.experimental import pallas as pl
from jax.experimental.pallas import tpu as pltpu
from jax.sharding import PartitionSpec as P

HEAD_SIZE = 128
AXES = ("seqa", "seqb")
MESH = pl.DeviceIdType.MESH
HIDDEN = -1e30


def kernel(
    sizes,
    starts_ref,
    queries_ref,
    keys_ref,
    values_ref,
    keys_hbm,
    values_hbm,
    out_ref,
    received,
    values_t,
    scores,
    weights,
    key_marks,
    query_marks,
    edge_bias,
    diag_bias,
    send_sem,
    recv_sem,
):
    across, inner, heads, group, rows, block = sizes
    devices = across * inner
    head = HEAD_SIZE
    blocks = rows // block
    tiles = 2 * blocks + 1
    step = pl.program_id(0)
    me = lax.axis_index("seqa") * inner + lax.axis_index("seqb")
    parity = lax.rem(me, 2)

    def place(shift):
        target = lax.rem(me + shift + devices, devices)
        return (target // inner, lax.rem(target, inner))

    def send(which, kind, h, source, target):
        return pltpu.make_async_remote_copy(
            src_ref=source,
            dst_ref=received.at[kind, h, pl.ds(which * rows, rows), :],
            send_sem=send_sem.at[which, kind, h],
            recv_sem=recv_sem.at[which, kind, h],
            device_id=target,
            device_id_type=MESH,
        )

    def own(kind, h):
        ref = values_hbm if kind else keys_hbm
        return ref.at[:, pl.ds(pl.multiple_of(h * head, head), head)]

    def landed(which, kind, h):
        return received.at[kind, h, pl.ds(which * rows, rows), :]

    @pl.when(step == 0)
    def _():
        barrier = pltpu.get_barrier_semaphore()
        for shift in (-2, -1, 1, 2):
            pl.semaphore_signal(barrier, inc=1, device_id=place(shift), device_id_type=MESH)
        pl.semaphore_wait(barrier, 4)

        def start_all(h, carry):
            for kind in range(2):
                send(0, kind, h, own(kind, h), place(2)).start()

            @pl.when(parity == 0)
            def _():
                for kind in range(2):
                    send(1, kind, h, own(kind, h), place(1)).start()

            return carry

        lax.fori_loop(0, heads, start_all, 0)

        key_at = lax.broadcasted_iota(jnp.int32, (block, block), 0)
        query_at = lax.broadcasted_iota(jnp.int32, (block, block), 1)
        edge_bias[...] = jnp.where(key_at > query_at, 0.0, HIDDEN)
        lane = lax.broadcasted_iota(jnp.int32, (block, head), 1)
        row = lax.broadcasted_iota(jnp.int32, (block, head), 0)
        for b in range(blocks):
            base = me * rows + b * block
            start = starts_ref[0:1, b * block : (b + 1) * block]
            diag_bias[b] = jnp.where(
                (key_at <= query_at) & (key_at + base >= start), 0.0, HIDDEN
            )
            first = jnp.broadcast_to(start[:, 0:1], (block, head))
            other = jnp.broadcast_to(jnp.where(start > base, 1.0, 0.0), (head, block)).T
            marks = jnp.where(lane == 0, 1.0, jnp.where(lane == 1, other, 0.0)) * HIDDEN
            query_marks[b] = marks.astype(jnp.bfloat16)
            for t in range(tiles - 1):
                at = row + (base - 2 * rows + t * block)
                before = jnp.where(at < first, 1.0, 0.0)
                mark = jnp.where(lane == 0, before, jnp.where(lane == 1, 1.0, 0.0))
                key_marks[b, t] = mark.astype(jnp.bfloat16)
            key_marks[b, tiles - 1] = jnp.zeros((block, head), jnp.bfloat16)

    for kind in range(2):
        send(0, kind, step, own(kind, step), place(2)).wait_recv()

    @pl.when(parity == 1)
    def _():
        for kind in range(2):
            send(1, kind, step, landed(0, kind, step), place(-1)).start()

    for kind in range(2):
        send(1, kind, step, own(kind, step), place(1)).wait_recv()

    for b in range(2 * blocks):
        part = received[1, step, b * block : (b + 1) * block, :]
        values_t[:, b * block : (b + 1) * block] = part.T
    for b in range(blocks):
        part = values_ref[b * block : (b + 1) * block, :]
        values_t[:, (2 * blocks + b) * block : (2 * blocks + b + 1) * block] = part.T

    scale = math.log2(math.e) / math.sqrt(head)
    units = [(g, b) for b in range(blocks) for g in range(group)]

    def query_side(u):
        g, b = units[u]
        q = queries_ref[b * block : (b + 1) * block, g * head : (g + 1) * head]
        q = (q.astype(jnp.float32) * scale).astype(jnp.bfloat16)
        return jnp.concatenate([q, query_marks[b]], axis=1)

    def score_tile(u, t, q, top):
        g, b = units[u]
        at = b + t
        if at < 2 * blocks:
            k = received[0, step, at * block : (at + 1) * block, :]
        else:
            k = keys_ref[(at - 2 * blocks) * block : (at - 2 * blocks + 1) * block, :]
        k = jnp.concatenate([k, key_marks[b, t]], axis=1)
        s = lax.dot_general(k, q, (((1,), (1,)), ((), ())), preferred_element_type=jnp.float32)
        if t == 0:
            s = s + edge_bias[...]
        if t == tiles - 1:
            s = s + diag_bias[b]
        scores[u % 2, t * block : (t + 1) * block, :] = s
        partial = jnp.max(s.reshape(block // 8, 8, block), axis=0)
        return partial if top is None else jnp.maximum(top, partial)

    def weigh_tile(u, t, top, total):
        s = scores[u % 2, t * block : (t + 1) * block, :]
        p = jnp.exp2(s - top)
        weights[u % 2, t * block : (t + 1) * block, :] = p.astype(jnp.bfloat16)
        partial = jnp.sum(p.reshape(block // 8, 8, block), axis=0)
        return partial if total is None else total + partial

    def finish(u, total):
        g, b = units[u]
        v = values_t[:, b * block : (b + tiles) * block]
        summed = jnp.dot(v, weights[u % 2], preferred_element_type=jnp.float32)
        summed = summed / jnp.sum(total, axis=0, keepdims=True)
        out_ref[b * block : (b + 1) * block, g * head : (g + 1) * head] = summed.T.astype(
            jnp.bfloat16
        )

    top = None
    q = query_side(0)
    for t in range(tiles):
        top = score_tile(0, t, q, top)
    for u in range(len(units)):
        top_now = jnp.max(top, axis=0, keepdims=True)
        top, total = None, None
        last = u == len(units) - 1
        if not last:
            q = query_side(u + 1)
        for t in range(tiles):
            if not last:
                top = score_tile(u + 1, t, q, top)
            total = weigh_tile(u, t, top_now, total)
        finish(u, total)

    @pl.when(step == heads - 1)
    def _():
        def end_all(h, carry):
            for which in range(2):
                for kind in range(2):
                    send(which, kind, h, own(kind, h), place(2)).wait_send()
            return carry

        lax.fori_loop(0, heads, end_all, 0)


def local(mesh, queries, keys, values, doc_start):
    rows = queries.shape[0]
    head = HEAD_SIZE
    heads = keys.shape[1] // head
    group = queries.shape[1] // keys.shape[1]
    block = rows // 2
    blocks = rows // block
    tiles = 2 * blocks + 1
    sizes = (mesh.shape["seqa"], mesh.shape["seqb"], heads, group, rows, block)
    assert (sizes[0] * sizes[1]) % 2 == 0
    return pl.pallas_call(
        functools.partial(kernel, sizes),
        grid=(heads,),
        out_shape=jax.ShapeDtypeStruct(queries.shape, jnp.bfloat16),
        in_specs=[
            pl.BlockSpec((1, rows), lambda h: (0, 0)),
            pl.BlockSpec((rows, group * head), lambda h: (0, h)),
            pl.BlockSpec((rows, head), lambda h: (0, h)),
            pl.BlockSpec((rows, head), lambda h: (0, h)),
            pl.BlockSpec(memory_space=pl.ANY),
            pl.BlockSpec(memory_space=pl.ANY),
        ],
        out_specs=pl.BlockSpec((rows, group * head), lambda h: (0, h)),
        scratch_shapes=[
            pltpu.VMEM((2, heads, 2 * rows, head), jnp.bfloat16),
            pltpu.VMEM((head, 3 * rows), jnp.bfloat16),
            pltpu.VMEM((2, tiles * block, block), jnp.float32),
            pltpu.VMEM((2, tiles * block, block), jnp.bfloat16),
            pltpu.VMEM((blocks, tiles, block, head), jnp.bfloat16),
            pltpu.VMEM((blocks, block, head), jnp.bfloat16),
            pltpu.VMEM((block, block), jnp.float32),
            pltpu.VMEM((blocks, block, block), jnp.float32),
            pltpu.SemaphoreType.DMA((2, 2, heads)),
            pltpu.SemaphoreType.DMA((2, 2, heads)),
        ],
        compiler_params=pltpu.CompilerParams(
            collective_id=0,
            has_side_effects=True,
            dimension_semantics=("arbitrary",),
            vmem_limit_bytes=60 * 1024 * 1024,
        ),
    )(doc_start.reshape(1, rows), queries, keys, values, keys, values)


def solution(mesh):
    return jax.shard_map(
        functools.partial(local, mesh),
        mesh=mesh,
        in_specs=(P(AXES, None), P(AXES, None), P(AXES, None), P(AXES)),
        out_specs=P(AXES, None),
        check_vma=False,
    )
```

time: 213 us -> 65 us (0.31)
  the two profiles are of different devices: /device:TPU:8 before, /device:TPU:0 now
where the time goes in v1:
time: 65 us; the launch traced here: 64.8 us
  Pallas kernels  60.1 us (92%)
  local copies, waits for them, and re-layouts  4.7 us (7%)
    pallas_call x1, Pallas kernels, local(): pl.pallas_call(functools.partial(kernel, sizes), grid=(heads,), out_shape...  60.1 us
    unnamed x1, local copies, waits for them, and re-layouts  4.7 us

profile of v1, /device:TPU:0, one launch (start us, length us, event | category | flops | bytes accessed | tf_op | source)
XLA Modules:
  0.0 64.8 jit_solution(2185227261897255531)
XLA Ops:
  0.0 60.1 %shard_map.46 = bf16[512,4096]{1,0:T(8,128)(2,1)} custom-call(s32[1,512]{1,0:T(1,128)} %bitcast.1, bf16[512,4096]{1,0:T(8,128)(2,1)} %queries_ref.1, bf16[512,1024]{1,0:T(8,128)(2,1)} %keys_hbm.1, bf16[512,1024]{1,0:T(8,128)(2,1)} %values_hbm.1, bf16[512,1024]{1,0:T(8,128)(2,1)} %keys_hbm.1, bf16[512,1024]{1,0:T(8,128)(2,1)} %values_hbm.1), custom_call_target="tpu_custom_call" | custom-call | tf_op jit(solution)/shard_map/pallas_call | solution.py:206
  60.1 4.7 %copy.6 = bf16[512,4096]{1,0:T(8,128)(2,1)} copy(bf16[512,4096]{1,0:T(8,128)(2,1)} %shard_map.46) | data formatting | bytes 8388608

commit v2 on v1

--- a/solution.py
+++ b/solution.py
@@ -17,9 +17,7 @@
 def kernel(
     sizes,
     starts_ref,
-    queries_ref,
-    keys_ref,
-    values_ref,
+    queries_hbm,
     keys_hbm,
     values_hbm,
     out_ref,
@@ -31,8 +29,12 @@
     query_marks,
     edge_bias,
     diag_bias,
+    queries_in,
+    keys_in,
+    values_in,
     send_sem,
     recv_sem,
+    fetch_sem,
 ):
     across, inner, heads, group, rows, block = sizes
     devices = across * inner
@@ -64,25 +66,62 @@
     def landed(which, kind, h):
         return received.at[kind, h, pl.ds(which * rows, rows), :]
 
+    has = {0: me >= 2, 1: me >= 1}
+    feeds = {0: me + 2 < devices, 1: jnp.where(parity == 0, me + 1 < devices, me >= 2)}
+
+    def fetch(h):
+        at = pl.ds(pl.multiple_of(h * head, head), head)
+        wide = pl.ds(pl.multiple_of(h * group * head, group * head), group * head)
+        return (
+            pltpu.make_async_copy(queries_hbm.at[:, wide], queries_in.at[h], fetch_sem.at[0, h]),
+            pltpu.make_async_copy(keys_hbm.at[:, at], keys_in.at[h], fetch_sem.at[1, h]),
+            pltpu.make_async_copy(values_hbm.at[:, at], values_in.at[h], fetch_sem.at[2, h]),
+        )
+
     @pl.when(step == 0)
     def _():
         barrier = pltpu.get_barrier_semaphore()
-        for shift in (-2, -1, 1, 2):
-            pl.semaphore_signal(barrier, inc=1, device_id=place(shift), device_id_type=MESH)
-        pl.semaphore_wait(barrier, 4)
+        near = ((-2, me >= 2), (-1, me >= 1), (1, me + 1 < devices), (2, me + 2 < devices))
+        for shift, there in near:
+
+            @pl.when(there)
+            def _():
+                pl.semaphore_signal(barrier, inc=1, device_id=place(shift), device_id_type=MESH)
+
+        count = sum(there.astype(jnp.int32) for _, there in near)
+        pl.semaphore_wait(barrier, count)
 
         def start_all(h, carry):
             for kind in range(2):
-                send(0, kind, h, own(kind, h), place(2)).start()
-
-            @pl.when(parity == 0)
+
+                @pl.when(feeds[0])
+                def _():
+                    send(0, kind, h, own(kind, h), place(2)).start()
+
+                @pl.when((parity == 0) & feeds[1])
+                def _():
+                    send(1, kind, h, own(kind, h), place(1)).start()
+
+            return carry
+
+        lax.fori_loop(0, heads, start_all, 0)
+
+        def fetch_all(h, carry):
+            for copy in fetch(h):
+                copy.start()
+            return carry
+
+        lax.fori_loop(0, heads, fetch_all, 0)
+
+        for which in range(2):
+
+            @pl.when(jnp.logical_not(has[which]))
             def _():
                 for kind in range(2):
-                    send(1, kind, h, own(kind, h), place(1)).start()
-
-            return carry
-
-        lax.fori_loop(0, heads, start_all, 0)
+                    for h in range(heads):
+                        received[kind, h, which * rows : (which + 1) * rows, :] = jnp.zeros(
+                            (rows, head), jnp.bfloat16
+                        )
 
         key_at = lax.broadcasted_iota(jnp.int32, (block, block), 0)
         query_at = lax.broadcasted_iota(jnp.int32, (block, block), 1)
@@ -106,30 +145,29 @@
                 key_marks[b, t] = mark.astype(jnp.bfloat16)
             key_marks[b, tiles - 1] = jnp.zeros((block, head), jnp.bfloat16)
 
-    for kind in range(2):
-        send(0, kind, step, own(kind, step), place(2)).wait_recv()
-
-    @pl.when(parity == 1)
-    def _():
-        for kind in range(2):
+    def arrive(kind):
+        @pl.when(has[0])
+        def _():
+            send(0, kind, step, own(kind, step), place(2)).wait_recv()
+
+        @pl.when((parity == 1) & has[0])
+        def _():
             send(1, kind, step, landed(0, kind, step), place(-1)).start()
 
-    for kind in range(2):
-        send(1, kind, step, own(kind, step), place(1)).wait_recv()
-
-    for b in range(2 * blocks):
-        part = received[1, step, b * block : (b + 1) * block, :]
-        values_t[:, b * block : (b + 1) * block] = part.T
-    for b in range(blocks):
-        part = values_ref[b * block : (b + 1) * block, :]
-        values_t[:, (2 * blocks + b) * block : (2 * blocks + b + 1) * block] = part.T
+        @pl.when(has[1])
+        def _():
+            send(1, kind, step, own(kind, step), place(1)).wait_recv()
+
+    for copy in fetch(step):
+        copy.wait()
+    arrive(0)
 
     scale = math.log2(math.e) / math.sqrt(head)
     units = [(g, b) for b in range(blocks) for g in range(group)]
 
     def query_side(u):
         g, b = units[u]
-        q = queries_ref[b * block : (b + 1) * block, g * head : (g + 1) * head]
+        q = queries_in[step, b * block : (b + 1) * block, g * head : (g + 1) * head]
         q = (q.astype(jnp.float32) * scale).astype(jnp.bfloat16)
         return jnp.concatenate([q, query_marks[b]], axis=1)
 
@@ -139,7 +177,7 @@
         if at < 2 * blocks:
             k = received[0, step, at * block : (at + 1) * block, :]
         else:
-            k = keys_ref[(at - 2 * blocks) * block : (at - 2 * blocks + 1) * block, :]
+            k = keys_in[step, (at - 2 * blocks) * block : (at - 2 * blocks + 1) * block, :]
         k = jnp.concatenate([k, key_marks[b, t]], axis=1)
         s = lax.dot_general(k, q, (((1,), (1,)), ((), ())), preferred_element_type=jnp.float32)
         if t == 0:
@@ -153,19 +191,19 @@
     def weigh_tile(u, t, top, total):
         s = scores[u % 2, t * block : (t + 1) * block, :]
         p = jnp.exp2(s - top)
-        weights[u % 2, t * block : (t + 1) * block, :] = p.astype(jnp.bfloat16)
+        weights[u, t * block : (t + 1) * block, :] = p.astype(jnp.bfloat16)
         partial = jnp.sum(p.reshape(block // 8, 8, block), axis=0)
         return partial if total is None else total + partial
 
     def finish(u, total):
         g, b = units[u]
         v = values_t[:, b * block : (b + tiles) * block]
-        summed = jnp.dot(v, weights[u % 2], preferred_element_type=jnp.float32)
-        summed = summed / jnp.sum(total, axis=0, keepdims=True)
-        out_ref[b * block : (b + 1) * block, g * head : (g + 1) * head] = summed.T.astype(
-            jnp.bfloat16
-        )
-
+        summed = jnp.dot(v, weights[u], preferred_element_type=jnp.float32)
+        summed = summed * total
+        at = pl.ds(pl.multiple_of((step * group + g) * head, head), head)
+        out_ref[b * block : (b + 1) * block, at] = summed.T.astype(jnp.bfloat16)
+
+    totals = []
     top = None
     q = query_side(0)
     for t in range(tiles):
@@ -180,14 +218,28 @@
             if not last:
                 top = score_tile(u + 1, t, q, top)
             total = weigh_tile(u, t, top_now, total)
-        finish(u, total)
+        totals.append(1.0 / jnp.sum(total, axis=0, keepdims=True))
+
+    arrive(1)
+    for b in range(3 * blocks):
+        if b < 2 * blocks:
+            part = received[1, step, b * block : (b + 1) * block, :]
+        else:
+            part = values_in[step, (b - 2 * blocks) * block : (b - 2 * blocks + 1) * block, :]
+        values_t[:, b * block : (b + 1) * block] = part.T
+    for u in range(len(units)):
+        finish(u, totals[u])
 
     @pl.when(step == heads - 1)
     def _():
         def end_all(h, carry):
             for which in range(2):
-                for kind in range(2):
-                    send(which, kind, h, own(kind, h), place(2)).wait_send()
+
+                @pl.when(feeds[which])
+                def _():
+                    for kind in range(2):
+                        send(which, kind, h, own(kind, h), place(1)).wait_send()
+
             return carry
 
         lax.fori_loop(0, heads, end_all, 0)
@@ -206,35 +258,37 @@
     return pl.pallas_call(
         functools.partial(kernel, sizes),
         grid=(heads,),
-        out_shape=jax.ShapeDtypeStruct(queries.shape, jnp.bfloat16),
+        out_shape=pltpu.VMEM(queries.shape, jnp.bfloat16),
         in_specs=[
             pl.BlockSpec((1, rows), lambda h: (0, 0)),
-            pl.BlockSpec((rows, group * head), lambda h: (0, h)),
-            pl.BlockSpec((rows, head), lambda h: (0, h)),
-            pl.BlockSpec((rows, head), lambda h: (0, h)),
+            pl.BlockSpec(memory_space=pl.ANY),
             pl.BlockSpec(memory_space=pl.ANY),
             pl.BlockSpec(memory_space=pl.ANY),
         ],
-        out_specs=pl.BlockSpec((rows, group * head), lambda h: (0, h)),
+        out_specs=pl.BlockSpec(memory_space=pltpu.VMEM),
         scratch_shapes=[
             pltpu.VMEM((2, heads, 2 * rows, head), jnp.bfloat16),
             pltpu.VMEM((head, 3 * rows), jnp.bfloat16),
             pltpu.VMEM((2, tiles * block, block), jnp.float32),
-            pltpu.VMEM((2, tiles * block, block), jnp.bfloat16),
+            pltpu.VMEM((group * blocks, tiles * block, block), jnp.bfloat16),
             pltpu.VMEM((blocks, tiles, block, head), jnp.bfloat16),
             pltpu.VMEM((blocks, block, head), jnp.bfloat16),
             pltpu.VMEM((block, block), jnp.float32),
             pltpu.VMEM((blocks, block, block), jnp.float32),
+            pltpu.VMEM((heads, rows, group * head), jnp.bfloat16),
+            pltpu.VMEM((heads, rows, head), jnp.bfloat16),
+            pltpu.VMEM((heads, rows, head), jnp.bfloat16),
             pltpu.SemaphoreType.DMA((2, 2, heads)),
             pltpu.SemaphoreType.DMA((2, 2, heads)),
+            pltpu.SemaphoreType.DMA((3, heads)),
         ],
         compiler_params=pltpu.CompilerParams(
             collective_id=0,
             has_side_effects=True,
             dimension_semantics=("arbitrary",),
-            vmem_limit_bytes=60 * 1024 * 1024,
+            vmem_limit_bytes=59 * 1024 * 1024,
         ),
-    )(doc_start.reshape(1, rows), queries, keys, values, keys, values)
+    )(doc_start.reshape(1, rows), queries, keys, values)
 
 
 def solution(mesh):

time: 65 us -> 55.5 us (0.85)
  the two profiles are of different devices: /device:TPU:0 before, /device:TPU:8 now
where the time goes in v2:
time: 55.5 us; the launch traced here: 55.3 us
  Pallas kernels  53.3 us (96%)
  local copies, waits for them, and re-layouts  2.02 us (4%)
    pallas_call x1, Pallas kernels, local(): pl.pallas_call(functools.partial(kernel, sizes), grid=(heads,), out_shape...  53.3 us
    unnamed x1, local copies, waits for them, and re-layouts  2.02 us

profile of v2, /device:TPU:8, one launch (start us, length us, event | category | flops | bytes accessed | tf_op | source)
XLA Modules:
  0.0 55.3 jit_solution(10416738349986454204)
XLA Ops:
  0.0 53.3 %shard_map.46 = bf16[512,4096]{1,0:T(8,128)(2,1)S(1)} custom-call(s32[1,512]{1,0:T(1,128)} %bitcast.1, bf16[512,4096]{1,0:T(8,128)(2,1)} %queries_hbm.1, bf16[512,1024]{1,0:T(8,128)(2,1)} %keys_hbm.1, bf16[512,1024]{1,0:T(8,128)(2,1)} %values_hbm.1), custom_call_target="tpu_custom_call" | custom-call | tf_op jit(solution)/shard_map/pallas_call | solution.py:258
  53.3 2.0 %copy.6 = bf16[512,4096]{1,0:T(8,128)(2,1)} copy(bf16[512,4096]{1,0:T(8,128)(2,1)S(1)} %shard_map.46) | data formatting | bytes 8388608
